TPU v7x, 512 devices: a whole 4x8x8 slice. The times are simulated.
512 devices in a mesh: space: 64 (over y_lo, z, x), tensor: 8 (over y_hi, core).
Axes of the slice: x: 4, y: 8 (y_hi: 4, y_lo: 2; y = y_hi * 2 + y_lo), z: 8, core: 2. Of those that a mesh axis runs over, the one named last changes fastest.
Arguments:
- tokens: float32 [2, 128, 128, 2048], P(None, 'space', None, 'tensor'), may hold values from -6 to 6
- in_gain: float32 [2048], replicated, may hold values from 0.25 to 1.75
- w_inner: bfloat16 [2048, 3072], P(None, 'tensor'), may hold values from -0.125 to 0.125
- w_bc: bfloat16 [2048, 256], replicated, may hold values from -0.03125 to 0.03125
- w_step: bfloat16 [2048, 48], P(None, 'tensor'), may hold values from -0.125 to 0.125
- step_bias: float32 [48], P('tensor'), may hold values from -3 to 0
- decay_rate: float32 [48], P('tensor'), may hold values from 0.02 to 2
- skip: float32 [48], P('tensor'), may hold values from 0.5 to 2
- norm_gain: float32 [3072], P('tensor'), may hold values from 0.25 to 1.75
- w_out: bfloat16 [3072, 2048], P('tensor'), may hold values from -0.109375 to 0.109375
Outputs:
- mixed: bfloat16 [2, 128, 128, 2048], P(None, 'space', None, 'tensor')
All inputs are finite; a program needn't handle non-finite values.
Results may differ from a plain program's by a relative error of at most 0.011.
Values may be sent and summed in bfloat16 or wider, within the bound.
No kernel may reach another device: no remote copies, remote signals or barrier semaphores. Data moves between devices by JAX's collectives and lax.ppermute only.
A program may use at most 64 MiB of HBM per device.

v0:
```python
import jax
import jax.numpy as jnp
from jax import lax
from jax.sharding import PartitionSpec as P

HEAD_DIM = 64
STATE = 128
NORM_HEADS = 6
EPS = 1e-05


def kernel(logdecay):
    running = jnp.cumsum(logdecay, axis=-1)
    length = logdecay.shape[-1]
    place = jnp.arange(length)
    lower = place[:, None] >= place[None, :]
    upper = place[:, None] <= place[None, :]
    later = running[..., :, None] - running[..., None, :]
    shifted = running - logdecay
    earlier = shifted[..., None, :] - shifted[..., :, None]
    forward = jnp.exp(jnp.where(lower, later, -jnp.inf))
    backward = jnp.exp(jnp.where(upper, earlier, -jnp.inf))
    return forward + backward


def scan_grid(values, maps, logdecay, along_rows):
    heads = logdecay.shape[-1]
    in_map = maps[..., :STATE]
    out_map = maps[..., STATE:]
    split_values = values.reshape(values.shape[:3] + (heads, HEAD_DIM))
    if along_rows:
        scores = jnp.einsum("ialn,iamn->ialm", out_map, in_map, preferred_element_type=jnp.float32)
        decays = jnp.moveaxis(logdecay.astype(jnp.float32), 3, 2)
    else:
        scores = jnp.einsum("ilan,iman->ialm", out_map, in_map, preferred_element_type=jnp.float32)
        decays = jnp.transpose(logdecay.astype(jnp.float32), (0, 2, 3, 1))
    weights = (scores[:, :, None] * kernel(decays)).astype(jnp.bfloat16)
    if along_rows:
        result = jnp.einsum(
            "iahlm,iamhp->ialhp", weights, split_values, preferred_element_type=jnp.float32
        )
    else:
        result = jnp.einsum(
            "iahlm,imahp->ilahp", weights, split_values, preferred_element_type=jnp.float32
        )
    return result.reshape(values.shape)


def on_device(
    tokens, in_gain, w_inner, w_bc, w_step, step_bias, decay_rate, skip, norm_gain, w_out
):
    whole = lax.all_gather(tokens.astype(jnp.bfloat16), "tensor", axis=3, tiled=True)
    rounded = whole.astype(jnp.float32)
    scale = lax.rsqrt(jnp.mean(rounded * rounded, axis=-1, keepdims=True) + EPS)
    normed = (rounded * scale * in_gain).astype(jnp.bfloat16)
    inner = jnp.einsum("irwd,dc->irwc", normed, w_inner, preferred_element_type=jnp.float32).astype(
        jnp.bfloat16
    )
    maps = jnp.einsum("irwd,dc->irwc", normed, w_bc, preferred_element_type=jnp.float32).astype(
        jnp.bfloat16
    )
    step = jax.nn.softplus(
        jnp.einsum("irwd,dc->irwc", normed, w_step, preferred_element_type=jnp.float32) + step_bias
    )
    logdecay = (-decay_rate * step).astype(jnp.bfloat16)
    heads_local = w_step.shape[1]
    lead = inner.shape[:3]
    value = (
        (inner.reshape(lead + (heads_local, HEAD_DIM)).astype(jnp.float32) * step[..., None])
        .reshape(inner.shape)
        .astype(jnp.bfloat16)
    )
    col_value = lax.all_to_all(value, "space", split_axis=2, concat_axis=1, tiled=True)
    col_maps = lax.all_to_all(maps, "space", split_axis=2, concat_axis=1, tiled=True)
    col_decay = lax.all_to_all(logdecay, "space", split_axis=2, concat_axis=1, tiled=True)
    column_out = scan_grid(col_value, col_maps, col_decay, False).astype(jnp.bfloat16)
    column_back = lax.all_to_all(column_out, "space", split_axis=1, concat_axis=2, tiled=True)
    row_out = scan_grid(value, maps, logdecay, True)
    skip_wide = jnp.repeat(skip, HEAD_DIM)
    total = row_out + column_back.astype(jnp.float32) + skip_wide * inner.astype(jnp.float32)
    group = NORM_HEADS * HEAD_DIM
    grouped = total.reshape(lead + (inner.shape[3] // group, group))
    norm_scale = lax.rsqrt(jnp.mean(grouped * grouped, axis=-1, keepdims=True) + EPS)
    gated = ((grouped * norm_scale).reshape(inner.shape) * norm_gain).astype(jnp.bfloat16)
    partial_out = jnp.einsum("irwc,cd->irwd", gated, w_out, preferred_element_type=jnp.float32)
    mixer = lax.psum_scatter(partial_out, "tensor", scatter_dimension=3, tiled=True)
    return (tokens + mixer).astype(jnp.bfloat16)


def solution(mesh):
    return jax.shard_map(
        on_device,
        mesh=mesh,
        in_specs=(
            P(None, "space", None, "tensor"),
            P(),
            P(None, "tensor"),
            P(),
            P(None, "tensor"),
            P("tensor"),
            P("tensor"),
            P("tensor"),
            P("tensor"),
            P("tensor", None),
        ),
        out_specs=P(None, "space", None, "tensor"),
        check_vma=False,
    )
```

profile of v0, /device:TPU:19, one launch (start us, length us, event | category | flops | bytes accessed | tf_op | source)
XLA Modules:
  0.0 218.5 jit_solution(5063790395113188788)
XLA Ops:
  6.6 1.9 convert_element_type.76
  8.5 0.7 neg.11
  9.2 45.6 %all-gather.2.cloned.1.call-done = bf16[2,2,128,2048]{3,2,1,0:T(8,128)(2,1)} async-done(((bf16[2,2,128,256]{3,2,1,0:T(8,128)(2,1)}), bf16[2,2,128,2048]{3,2,1,0:T(8,128)(2,1)}) %all-gather.2.cloned.1.call-update) | async-done | bytes 2097168 | tf_op jit(solution)/shard_map/all_gather | solution.py:52
  54.7 2.2 %fusion = f32[2,2,128]{2,1,0:T(2,128)S(1)} fusion(bf16[2,2,128,2048]{3,2,1,0:T(8,128)(2,1)} %all-gather.2.cloned.1.call-done), kind=kLoop, calls=%fused_computation.2 | loop fusion | flops 3145216 | bytes 2099200 | tf_op jit(solution)/shard_map/reduce_sum | solution.py:54
  57.0 0.8 multiply_convert_fusion.7
  57.8 0.8 copy.52
  58.6 12.8 %all-to-all-start.2 = ((bf16[2,2,128,6]{3,1,0,2:T(2,128)(2,1)}), bf16[2,2,128,6]{3,1,0,2:T(2,128)(2,1)S(1)}, u32[]{:S(2)}, u32[]{:S(2)}) async-start(bf16[2,2,128,6]{3,1,0,2:T(2,128)(2,1)} %copy.52), calls=%async_computation.2 | async-start | bytes 262144 | tf_op jit(solution)/shard_map/all_to_all | solution.py:75
  71.5 2.4 %convolution_convert_fusion.1 = bf16[2,2,128,256]{3,2,1,0:T(8,128)(2,1)S(1)} fusion(bf16[2,2,128,2048]{3,2,1,0:T(8,128)(2,1)} %all-gather.2.cloned.1.call-done, f32[2048]{0:T(1024)S(1)} %copy-done.13, f32[2,2,128]{2,1,0:T(2,128)S(1)} %add_rsqrt_fusion.1, bf16[2048,256]{1,0:T(8,128)(2,1)S(1)} %copy-done.11), kind=kOutput, calls=%fused_computation.14 | convolution fusion | flops 541196288 | bytes 3418112 | tf_op jit(solution)/shard_map/irwd,dc->irwc/dot_general | solution.py:59
  73.8 1.0 copy.48
  74.8 5.6 %all-to-all-done.2 = bf16[2,2,128,6]{3,1,0,2:T(2,128)(2,1)S(1)} async-done(((bf16[2,2,128,6]{3,1,0,2:T(2,128)(2,1)}), bf16[2,2,128,6]{3,1,0,2:T(2,128)(2,1)S(1)}, u32[]{:S(2)}, u32[]{:S(2)}) %all-to-all-start.2) | async-done | bytes 6176 | tf_op jit(solution)/shard_map/all_to_all | solution.py:75
  80.5 6.1 %all-to-all-start.1 = ((bf16[2,2,128,256]{3,1,0,2:T(2,128)(2,1)}), bf16[2,2,128,256]{3,1,0,2:T(2,128)(2,1)S(1)}, u32[]{:S(2)}, u32[]{:S(2)}) async-start(bf16[2,2,128,256]{3,1,0,2:T(2,128)(2,1)} %copy.48), calls=%async_computation.1 | async-start | bytes 524288 | tf_op jit(solution)/shard_map/all_to_all | solution.py:74
  86.6 0.1 broadcast_in_dim.25
  86.6 0.7 mul.106
  87.4 1.2 copy.44
  88.5 4.4 %multiply_convert_fusion.5 = (bf16[2,2,128,384]{3,2,1,0:T(8,128)(2,1)S(1)}, f32[2,2,128,384]{3,2,1,0:T(8,128)}) fusion(f32[2,2,128,384]{3,2,1,0:T(8,128)} %copy.44, bf16[2048,384]{1,0:T(8,128)(2,1)} %param.12, bf16[2,2,128,2048]{3,2,1,0:T(8,128)(2,1)} %all-gather.2.cloned.1.call-done, f32[2048]{0:T(1024)S(1)} %copy-done.13, ...), kind=kOutput, calls=%fused_computation.34 | convolution fusion | flops 810287104 | bytes 5646336 | tf_op jit(solution)/shard_map/irwd,dc->irwc/dot_general | solution.py:56
  92.9 1.1 copy.46
  94.1 2.0 all-to-all-done.1
  96.1 8.8 %all-to-all-start = ((bf16[2,2,128,384]{3,1,0,2:T(2,128)(2,1)}), bf16[2,2,128,384]{3,1,0,2:T(2,128)(2,1)S(1)}, u32[]{:S(2)}, u32[]{:S(2)}) async-start(bf16[2,2,128,384]{3,1,0,2:T(2,128)(2,1)} %copy.46), calls=%async_computation | async-start | bytes 786432 | tf_op jit(solution)/shard_map/all_to_all | solution.py:73
  104.8 0.6 iota_compare_fusion
  105.5 0.1 copy.53
  105.6 0.2 copy.54
  105.7 0.2 copy.55
  105.9 0.1 copy.56
  106.1 1.1 reduce_window_sum.18
  107.2 0.6 bitcast_subtract_fusion
  107.8 0.2 copy.49
  108.0 0.2 fusion.53
  108.2 0.2 fusion.40
  108.4 6.6 %all-to-all-done = bf16[2,2,128,384]{3,1,0,2:T(2,128)(2,1)S(1)} async-done(((bf16[2,2,128,384]{3,1,0,2:T(2,128)(2,1)}), bf16[2,2,128,384]{3,1,0,2:T(2,128)(2,1)S(1)}, u32[]{:S(2)}, u32[]{:S(2)}) %all-to-all-start) | async-done | bytes 393248 | tf_op jit(solution)/shard_map/all_to_all | solution.py:73
  115.0 0.3 copy.77
  115.3 1.6 reshape.67
  116.9 2.5 %convolution_convert_fusion = bf16[2,2,6,64,128]{4,3,2,1,0:T(8,128)(2,1)S(1)} fusion(bf16[2,128,2,6,64]{4,3,2,1,0:T(8,128)(2,1)} %reshape.67, f32[2,2,6,128]{3,2,1,0:T(8,128)} %bitcast_subtract_fusion, f32[2,2,6,128]{3,2,1,0:T(8,128)} %copy-done.3, f32[2,2,128,128]{3,2,1,0:T(8,128)S(1)} %fusion.40, pred[128,128]{1,0:T(8,128)(4,1)} %get-tuple-element.14, ...), kind=kOutput, calls=%fused_computation.13 | convolution fusion | flops 53280768 | bytes 1105920 | tf_op jit(solution)/shard_map/iahlm,imahp->ilahp/dot_general | solution.py:43
  119.4 1.1 copy.58
  120.5 10.5 %all-to-all-start.3 = ((bf16[2,128,2,384]{3,2,0,1:T(2,128)(2,1)}), bf16[2,128,2,384]{3,2,0,1:T(2,128)(2,1)S(1)}, u32[]{:S(2)}, u32[]{:S(2)}) async-start(bf16[2,128,2,384]{3,2,0,1:T(2,128)(2,1)} %copy.58), calls=%async_computation.3 | async-start | bytes 786432 | tf_op jit(solution)/shard_map/all_to_all | solution.py:77
  131.0 0.2 reduce-scatter.2.cloned.1.call-start
  131.3 0.2 copy.45
  131.6 1.2 reduce_window_sum.17
  132.8 0.2 fusion.37
  133.0 2.0 fusion.17
  135.1 1.4 copy.62
  136.5 4.8 %all-to-all-done.3 = bf16[2,128,2,384]{3,2,0,1:T(2,128)(2,1)S(1)} async-done(((bf16[2,128,2,384]{3,2,0,1:T(2,128)(2,1)}), bf16[2,128,2,384]{3,2,0,1:T(2,128)(2,1)S(1)}, u32[]{:S(2)}, u32[]{:S(2)}) %all-to-all-start.3) | async-done | bytes 393248 | tf_op jit(solution)/shard_map/all_to_all | solution.py:77
  141.3 0.6 copy.60
  142.0 0.3 copy.61
  142.2 1.4 reshape.68
  143.7 1.6 multiply_reduce_fusion
  145.3 3.3 %fusion.3 = f32[2,2,128,2048]{3,2,1,0:T(8,128)} fusion(bf16[384,2048]{1,0:T(8,128)(2,1)S(1)} %copy-done, f32[2,2,128,384]{3,2,1,0:T(8,128)S(1)} %get-tuple-element.6, f32[384]{0:T(512)S(1)} %copy-done.7, f32[2,2,128]{2,1,0:T(2,128)S(1)} %add_rsqrt_fusion), kind=kOutput, calls=%fused_computation.5 | convolution fusion | flops 805896192 | bytes 6557184 | tf_op jit(solution)/shard_map/irwc,cd->irwd/dot_general | solution.py:85
  148.6 61.3 %reduce-scatter.2.cloned.1.call-done = f32[2,2,128,256]{3,2,1,0:T(8,128)} async-done(((f32[2,2,128,2048]{3,2,1,0:T(8,128)}), f32[2,2,128,256]{3,2,1,0:T(8,128)}) %reduce-scatter.2.cloned.1.call-update) | async-done | bytes 524304 | tf_op jit(solution)/shard_map/reduce_scatter | solution.py:86
  209.8 1.8 add_convert_fusion
  (39 shorter events, 0.4 us)
Async XLA Ops:
  6.5 138.7 %copy-start = (bf16[384,2048]{1,0:T(8,128)(2,1)S(1)}, bf16[384,2048]{1,0:T(8,128)(2,1)}, u32[]{:S(2)}) copy-start(bf16[384,2048]{1,0:T(8,128)(2,1)} %param.19) | copy-start | bytes 4718596
  6.5 50.4 %copy-start.13 = (f32[2048]{0:T(1024)S(1)}, f32[2048]{0:T(1024)}, u32[]{:S(2)}) copy-start(f32[2048]{0:T(1024)} %param.11) | copy-start | bytes 24580
  6.5 50.4 %copy-start.14 = (f32[6]{0:T(128)S(1)}, f32[6]{0:T(128)}, u32[]{:S(2)}) copy-start(f32[6]{0:T(128)} %param.15) | copy-start | bytes 76
  6.5 50.5 %copy-start.12 = (bf16[2048,6]{0,1:T(8,128)(2,1)S(1)}, bf16[2048,6]{0,1:T(8,128)(2,1)}, u32[]{:S(2)}) copy-start(bf16[2048,6]{0,1:T(8,128)(2,1)} %param.14) | copy-start | bytes 73732
  6.5 48.2 %all-gather.2.cloned.1.call-start = ((), (), s32[]{:S(2)}) async-start(), calls=%async_computation.5 | async-start | bytes 2359296 | tf_op jit(solution)/shard_map/all_gather | solution.py:52
  9.2 48.7 %copy-start.8 = (f32[6]{0:T(128)}, f32[6]{0:T(128)S(1)}, u32[]{:S(2)}) copy-start(f32[6]{0:T(128)S(1)} %neg.11) | copy-start | bytes 76
  54.7 2.3 %copy-start.1 = (bf16[2,2,128,2048]{3,2,1,0:T(8,128)(2,1)S(1)}, bf16[2,2,128,2048]{3,2,1,0:T(8,128)(2,1)}, u32[]{:S(2)}) copy-start(bf16[2,2,128,2048]{3,2,1,0:T(8,128)(2,1)} %all-gather.2.cloned.1.call-done) | copy-start | bytes 6291460
  57.0 14.4 %copy-start.11 = (bf16[2048,256]{1,0:T(8,128)(2,1)S(1)}, bf16[2048,256]{1,0:T(8,128)(2,1)}, u32[]{:S(2)}) copy-start(bf16[2048,256]{1,0:T(8,128)(2,1)} %param.13) | copy-start | bytes 3145732
  58.6 21.8 %all-to-all-start.2 = ((bf16[2,2,128,6]{3,1,0,2:T(2,128)(2,1)}), bf16[2,2,128,6]{3,1,0,2:T(2,128)(2,1)S(1)}, u32[]{:S(2)}, u32[]{:S(2)}) async-start(bf16[2,2,128,6]{3,1,0,2:T(2,128)(2,1)} %copy.52), calls=%async_computation.2 | async-start | bytes 262144 | tf_op jit(solution)/shard_map/all_to_all | solution.py:75
  71.5 15.1 %copy-start.10 = (f32[6]{0:T(128)S(1)}, f32[6]{0:T(128)}, u32[]{:S(2)}) copy-start(f32[6]{0:T(128)} %param.17) | copy-start | bytes 76
  80.5 15.6 %all-to-all-start.1 = ((bf16[2,2,128,256]{3,1,0,2:T(2,128)(2,1)}), bf16[2,2,128,256]{3,1,0,2:T(2,128)(2,1)S(1)}, u32[]{:S(2)}, u32[]{:S(2)}) async-start(bf16[2,2,128,256]{3,1,0,2:T(2,128)(2,1)} %copy.48), calls=%async_computation.1 | async-start | bytes 524288 | tf_op jit(solution)/shard_map/all_to_all | solution.py:74
  96.1 18.9 %all-to-all-start = ((bf16[2,2,128,384]{3,1,0,2:T(2,128)(2,1)}), bf16[2,2,128,384]{3,1,0,2:T(2,128)(2,1)S(1)}, u32[]{:S(2)}, u32[]{:S(2)}) async-start(bf16[2,2,128,384]{3,1,0,2:T(2,128)(2,1)} %copy.46), calls=%async_computation | async-start | bytes 786432 | tf_op jit(solution)/shard_map/all_to_all | solution.py:73
  107.2 7.8 %copy-start.3 = (f32[2,2,6,128]{3,2,1,0:T(8,128)}, f32[2,2,6,128]{3,2,1,0:T(8,128)S(1)}, u32[]{:S(2)}) copy-start(f32[2,2,6,128]{3,2,1,0:T(8,128)S(1)} %reduce_window_sum.18) | copy-start | bytes 36868
  119.4 11.9 %copy-start.9 = (f32[6]{0:T(128)S(1)}, f32[6]{0:T(128)}, u32[]{:S(2)}) copy-start(f32[6]{0:T(128)} %copy-done.8) | copy-start | bytes 76
  119.4 13.6 %copy-start.4 = (pred[128,128]{1,0:T(8,128)(4,1)S(1)}, pred[128,128]{1,0:T(8,128)(4,1)}, u32[]{:S(2)}) copy-start(pred[128,128]{1,0:T(8,128)(4,1)} %get-tuple-element.14) | copy-start | bytes 49156
  119.4 13.6 %copy-start.5 = (pred[128,128]{1,0:T(8,128)(4,1)S(1)}, pred[128,128]{1,0:T(8,128)(4,1)}, u32[]{:S(2)}) copy-start(pred[128,128]{1,0:T(8,128)(4,1)} %get-tuple-element.15) | copy-start | bytes 49156
  120.5 20.8 %all-to-all-start.3 = ((bf16[2,128,2,384]{3,2,0,1:T(2,128)(2,1)}), bf16[2,128,2,384]{3,2,0,1:T(2,128)(2,1)S(1)}, u32[]{:S(2)}, u32[]{:S(2)}) async-start(bf16[2,128,2,384]{3,2,0,1:T(2,128)(2,1)} %copy.58), calls=%async_computation.3 | async-start | bytes 786432 | tf_op jit(solution)/shard_map/all_to_all | solution.py:77
  131.0 78.8 %reduce-scatter.2.cloned.1.call-start = ((), (), s32[]{:S(2)}) async-start(), calls=%async_computation.6 | async-start | bytes 4718592 | tf_op jit(solution)/shard_map/reduce_scatter | solution.py:86
  141.9 1.7 copy-start.6
  143.7 1.6 copy-start.7
  148.6 61.3 %copy-start.2 = (f32[2,2,128,256]{3,2,1,0:T(8,128)S(1)}, f32[2,2,128,256]{3,2,1,0:T(8,128)}, u32[]{:S(2)}) copy-start(f32[2,2,128,256]{3,2,1,0:T(8,128)} %param.10) | copy-start | bytes 1572868
Sparse Core Ops, SparseCore 0:
  9.5 45.2 all-gather.1
  148.7 61.0 reduce-scatter.1
where the time goes:
time: 219 us; the launch traced here: 218 us
  waiting for transfers between devices  126 us (58%)
  starting transfers between devices  38.4 us (18%)
  matrix products  15.8 us (7%)
  between operations  13.7 us (6%)
  local copies, waits for them, and re-layouts  12.8 us (6%)
  other arithmetic  11.9 us (5%)
    reduce_scatter x1, waiting for transfers between devices, on_device(): lax.psum_scatter(partial_out, 'tensor', scatter_dimension=3, tiled=True)  61.3 us
    all_gather x1, waiting for transfers between devices, on_device(): lax.all_gather(tokens.astype(jnp.bfloat16), 'tensor', axis=3, tiled=True)  45.6 us
    all_to_all x1, starting transfers between devices, on_device(): lax.all_to_all(logdecay, 'space', split_axis=2, concat_axis=1, tiled=True)  12.8 us
    all_to_all x1, starting transfers between devices, on_device(): lax.all_to_all(column_out, 'space', split_axis=1, concat_axis=2, tiled=True)  10.5 us
    all_to_all x1, starting transfers between devices, on_device(): lax.all_to_all(value, 'space', split_axis=2, concat_axis=1, tiled=True)  8.77 us
    all_to_all x1, waiting for transfers between devices, on_device(): lax.all_to_all(value, 'space', split_axis=2, concat_axis=1, tiled=True)  6.57 us
    all_to_all x1, starting transfers between devices, on_device(): lax.all_to_all(maps, 'space', split_axis=2, concat_axis=1, tiled=True)  6.09 us
    all_to_all x1, waiting for transfers between devices, on_device(): lax.all_to_all(logdecay, 'space', split_axis=2, concat_axis=1, tiled=True)  5.64 us
  transfers between devices with their start and end apart: 6, of which 6 were waited for; matrix products, arithmetic and copies ran while one was open for 9% of the time, Pallas kernels for 0%

commit v1 on v0

--- a/solution.py
+++ b/solution.py
@@ -49,7 +49,9 @@
 def on_device(
     tokens, in_gain, w_inner, w_bc, w_step, step_bias, decay_rate, skip, norm_gain, w_out
 ):
-    whole = lax.all_gather(tokens.astype(jnp.bfloat16), "tensor", axis=3, tiled=True)
+    part = tokens.astype(jnp.bfloat16)
+    parts = lax.all_gather(part, "tensor", axis=0, tiled=False)
+    whole = jnp.concatenate(parts, axis=3)
     rounded = whole.astype(jnp.float32)
     scale = lax.rsqrt(jnp.mean(rounded * rounded, axis=-1, keepdims=True) + EPS)
     normed = (rounded * scale * in_gain).astype(jnp.bfloat16)

time: 219 us -> 217 us (level)
  starting transfers between devices: 38.4 us -> 36.1 us
    all_gather x1, waiting for transfers between devices: 45.6 us -> 43.3 us  [on_device(): parts = lax.all_gather(part, 'tensor', axis=0, tiled=False)]
  transfers between devices with their start and end apart: 6 -> 6, of which waited for: 6 -> 6; matrix products, arithmetic and copies ran while one was open for 9% -> 8% of each run, Pallas kernels for 0% -> 0%
where the time goes in v1:
time: 217 us
  waiting for transfers between devices  125 us (58%)
  starting transfers between devices  36.1 us (17%)
  matrix products  15.4 us (7%)
  local copies, waits for them, and re-layouts  13.8 us (6%)
  between operations  13.7 us (6%)
  other arithmetic  12.2 us (6%)
    reduce_scatter x1, waiting for transfers between devices, on_device(): lax.psum_scatter(partial_out, 'tensor', scatter_dimension=3, tiled=True)  61.2 us
    all_gather x1, waiting for transfers between devices, on_device(): parts = lax.all_gather(part, 'tensor', axis=0, tiled=False)  43.3 us
    all_to_all x1, starting transfers between devices, on_device(): lax.all_to_all(logdecay, 'space', split_axis=2, concat_axis=1, tiled=True)  10.9 us
    all_to_all x1, starting transfers between devices, on_device(): lax.all_to_all(column_out, 'space', split_axis=1, concat_axis=2, tiled=True)  10.6 us
    all_to_all x1, starting transfers between devices, on_device(): lax.all_to_all(value, 'space', split_axis=2, concat_axis=1, tiled=True)  8.27 us
    all_to_all x1, waiting for transfers between devices, on_device(): lax.all_to_all(column_out, 'space', split_axis=1, concat_axis=2, tiled=True)  6.45 us
    all_to_all x1, starting transfers between devices, on_device(): lax.all_to_all(maps, 'space', split_axis=2, concat_axis=1, tiled=True)  6.27 us
    all_to_all x1, waiting for transfers between devices, on_device(): lax.all_to_all(value, 'space', split_axis=2, concat_axis=1, tiled=True)  6.2 us
  transfers between devices with their start and end apart: 6, of which 6 were waited for; matrix products, arithmetic and copies ran while one was open for 8% of the time, Pallas kernels for 0%

profile of v1, /device:TPU:19, one launch (start us, length us, event | category | flops | bytes accessed | tf_op | source)
XLA Modules:
  0.0 216.6 jit_solution(8658991779919762531)
XLA Ops:
  6.5 1.9 convert_element_type.86
  8.5 0.7 neg.11
  9.1 43.3 %all-gather.3.cloned.1.call-done = bf16[16,2,128,256]{3,2,1,0:T(8,128)(2,1)} async-done(((bf16[2,2,128,256]{3,2,1,0:T(8,128)(2,1)}), bf16[16,2,128,256]{3,2,1,0:T(8,128)(2,1)}) %all-gather.3.cloned.1.call-update) | async-done | bytes 2097168 | tf_op jit(solution)/shard_map/all_gather | solution.py:53
  52.5 2.2 %fusion = f32[2,2,128]{2,1,0:T(2,128)S(1)} fusion(bf16[8,2,2,128,256]{4,3,2,1,0:T(8,128)(2,1)} %bitcast.85), kind=kLoop, calls=%fused_computation.2 | loop fusion | flops 3145216 | bytes 2099200 | tf_op jit(solution)/shard_map/reduce_sum | solution.py:56
  54.7 0.5 convert_bitcast_fusion
  55.2 0.6 copy.73
  55.9 0.4 multiply_convert_fusion
  56.4 1.3 copy-done.1
  57.7 0.7 multiply_convert_fusion.8
  58.4 0.8 copy.56
  59.2 10.9 %all-to-all-start.2 = ((bf16[2,2,128,6]{3,1,0,2:T(2,128)(2,1)}), bf16[2,2,128,6]{3,1,0,2:T(2,128)(2,1)S(1)}, u32[]{:S(2)}, u32[]{:S(2)}) async-start(bf16[2,2,128,6]{3,1,0,2:T(2,128)(2,1)} %copy.56), calls=%async_computation.2 | async-start | bytes 262144 | tf_op jit(solution)/shard_map/all_to_all | solution.py:77
  70.2 2.6 %convolution_convert_fusion.1 = bf16[2,2,128,256]{3,2,1,0:T(8,128)(2,1)S(1)} fusion(bf16[2,2,128,2048]{3,2,1,0:T(8,128)(2,1)} %copy-done.1, bf16[2048,256]{1,0:T(8,128)(2,1)} %param.13), kind=kOutput, calls=%fused_computation.13 | convolution fusion | flops 537001984 | bytes 3407872 | tf_op jit(solution)/shard_map/irwd,dc->irwc/dot_general | solution.py:61
  72.7 1.0 copy.52
  73.7 5.4 %all-to-all-done.2 = bf16[2,2,128,6]{3,1,0,2:T(2,128)(2,1)S(1)} async-done(((bf16[2,2,128,6]{3,1,0,2:T(2,128)(2,1)}), bf16[2,2,128,6]{3,1,0,2:T(2,128)(2,1)S(1)}, u32[]{:S(2)}, u32[]{:S(2)}) %all-to-all-start.2) | async-done | bytes 6176 | tf_op jit(solution)/shard_map/all_to_all | solution.py:77
  79.1 6.3 %all-to-all-start.1 = ((bf16[2,2,128,256]{3,1,0,2:T(2,128)(2,1)}), bf16[2,2,128,256]{3,1,0,2:T(2,128)(2,1)}, u32[]{:S(2)}, u32[]{:S(2)}) async-start(bf16[2,2,128,256]{3,1,0,2:T(2,128)(2,1)} %copy.52), calls=%async_computation.1 | async-start | bytes 524288 | tf_op jit(solution)/shard_map/all_to_all | solution.py:76
  85.5 0.7 mul.108
  86.2 0.3 copy.48
  86.5 4.2 %multiply_convert_fusion.6 = (bf16[2,2,128,384]{3,2,1,0:T(8,128)(2,1)S(1)}, f32[2,2,128,384]{3,2,1,0:T(8,128)}) fusion(f32[2,2,128,384]{3,2,1,0:T(8,128)S(1)} %copy.48, bf16[2,2,128,2048]{3,2,1,0:T(8,128)(2,1)} %copy-done.1, bf16[2048,384]{1,0:T(8,128)(2,1)} %param.12), kind=kOutput, calls=%fused_computation.33 | convolution fusion | flops 806092800 | bytes 5636096 | tf_op jit(solution)/shard_map/irwd,dc->irwc/dot_general | solution.py:58
  90.7 1.2 copy.50
  91.8 2.8 %all-to-all-done.1 = bf16[2,2,128,256]{3,1,0,2:T(2,128)(2,1)} async-done(((bf16[2,2,128,256]{3,1,0,2:T(2,128)(2,1)}), bf16[2,2,128,256]{3,1,0,2:T(2,128)(2,1)}, u32[]{:S(2)}, u32[]{:S(2)}) %all-to-all-start.1) | async-done | bytes 262176 | tf_op jit(solution)/shard_map/all_to_all | solution.py:76
  94.7 8.3 %all-to-all-start = ((bf16[2,2,128,384]{3,1,0,2:T(2,128)(2,1)}), bf16[2,2,128,384]{3,1,0,2:T(2,128)(2,1)S(1)}, u32[]{:S(2)}, u32[]{:S(2)}) async-start(bf16[2,2,128,384]{3,1,0,2:T(2,128)(2,1)} %copy.50), calls=%async_computation | async-start | bytes 786432 | tf_op jit(solution)/shard_map/all_to_all | solution.py:75
  103.0 0.6 iota_compare_fusion
  103.7 0.2 copy.58
  103.9 0.2 copy.59
  104.1 0.1 copy.60
  104.2 1.1 reduce_window_sum.18
  105.3 1.2 copy.53
  106.5 0.2 fusion.48
  106.7 0.2 fusion.35
  106.9 6.2 %all-to-all-done = bf16[2,2,128,384]{3,1,0,2:T(2,128)(2,1)S(1)} async-done(((bf16[2,2,128,384]{3,1,0,2:T(2,128)(2,1)}), bf16[2,2,128,384]{3,1,0,2:T(2,128)(2,1)S(1)}, u32[]{:S(2)}, u32[]{:S(2)}) %all-to-all-start) | async-done | bytes 393248 | tf_op jit(solution)/shard_map/all_to_all | solution.py:75
  113.1 0.3 copy.82
  113.4 1.6 reshape.71
  115.0 2.5 %convolution_convert_fusion = bf16[2,2,6,64,128]{4,3,2,1,0:T(8,128)(2,1)S(1)} fusion(bf16[2,128,2,6,64]{4,3,2,1,0:T(8,128)(2,1)} %reshape.71, f32[2,2,6,128]{3,2,1,0:T(8,128)S(1)} %bitcast_subtract_fusion, f32[2,2,6,128]{3,2,1,0:T(8,128)S(1)} %reduce_window_sum.18, f32[2,2,128,128]{3,2,1,0:T(8,128)S(1)} %fusion.35, pred[128,128]{1,0:T(8,128)(4,1)S(1)} %copy-done.5, ...), kind=kOutput, calls=%fused_computation.12 | convolution fusion | flops 53280768 | bytes 1105920 | tf_op jit(solution)/shard_map/iahlm,imahp->ilahp/dot_general | solution.py:43
  117.5 1.1 copy.62
  118.6 10.6 %all-to-all-start.3 = ((bf16[2,128,2,384]{3,2,0,1:T(2,128)(2,1)}), bf16[2,128,2,384]{3,2,0,1:T(2,128)(2,1)S(1)}, u32[]{:S(2)}, u32[]{:S(2)}) async-start(bf16[2,128,2,384]{3,2,0,1:T(2,128)(2,1)} %copy.62), calls=%async_computation.3 | async-start | bytes 786432 | tf_op jit(solution)/shard_map/all_to_all | solution.py:79
  129.3 0.2 copy.49
  129.5 1.2 reduce_window_sum.17
  130.8 0.2 fusion.32
  131.0 1.8 fusion.12
  132.7 0.3 copy.66
  133.0 6.4 %all-to-all-done.3 = bf16[2,128,2,384]{3,2,0,1:T(2,128)(2,1)S(1)} async-done(((bf16[2,128,2,384]{3,2,0,1:T(2,128)(2,1)}), bf16[2,128,2,384]{3,2,0,1:T(2,128)(2,1)S(1)}, u32[]{:S(2)}, u32[]{:S(2)}) %all-to-all-start.3) | async-done | bytes 393248 | tf_op jit(solution)/shard_map/all_to_all | solution.py:79
  139.5 0.6 copy.64
  140.2 0.3 copy.65
  140.4 1.4 reshape.73
  141.9 1.6 multiply_reduce_fusion
  143.5 3.3 %fusion.1 = f32[2,2,128,2048]{3,2,1,0:T(8,128)} fusion(bf16[384,2048]{1,0:T(8,128)(2,1)S(1)} %copy-done, f32[2,2,128,384]{3,2,1,0:T(8,128)S(1)} %get-tuple-element.6, f32[384]{0:T(512)S(1)} %copy-done.11, f32[2,2,128]{2,1,0:T(2,128)S(1)} %add_rsqrt_fusion), kind=kOutput, calls=%fused_computation.4 | convolution fusion | flops 805896192 | bytes 6557184 | tf_op jit(solution)/shard_map/irwc,cd->irwd/dot_general | solution.py:87
  146.8 61.2 %reduce-scatter.2.cloned.1.call-done = f32[2,2,128,256]{3,2,1,0:T(8,128)} async-done(((f32[2,2,128,2048]{3,2,1,0:T(8,128)}), f32[2,2,128,256]{3,2,1,0:T(8,128)}) %reduce-scatter.2.cloned.1.call-update) | async-done | bytes 524304 | tf_op jit(solution)/shard_map/reduce_scatter | solution.py:88
  208.0 1.8 add_convert_fusion
  (40 shorter events, 0.6 us)
Async XLA Ops:
  6.5 136.9 %copy-start = (bf16[384,2048]{1,0:T(8,128)(2,1)S(1)}, bf16[384,2048]{1,0:T(8,128)(2,1)}, u32[]{:S(2)}) copy-start(bf16[384,2048]{1,0:T(8,128)(2,1)} %param.19) | copy-start | bytes 4718596
  6.5 45.9 %all-gather.3.cloned.1.call-start = ((), (), s32[]{:S(2)}) async-start(), calls=%async_computation.6 | async-start | bytes 2359296 | tf_op jit(solution)/shard_map/all_gather | solution.py:53
  9.1 47.3 %copy-start.7 = (f32[6]{0:T(128)}, f32[6]{0:T(128)S(1)}, u32[]{:S(2)}) copy-start(f32[6]{0:T(128)S(1)} %neg.11) | copy-start | bytes 76
  52.5 2.2 %copy-start.2 = (bf16[16,2,128,256]{3,2,1,0:T(8,128)(2,1)S(1)}, bf16[16,2,128,256]{3,2,1,0:T(8,128)(2,1)}, u32[]{:S(2)}) copy-start(bf16[16,2,128,256]{3,2,1,0:T(8,128)(2,1)} %all-gather.3.cloned.1.call-done) | copy-start | bytes 6291460
  55.2 0.7 copy-start.9
  55.9 1.8 copy-start.4
  55.9 1.8 copy-start.12
  56.4 1.3 copy-start.1
  59.2 19.9 %all-to-all-start.2 = ((bf16[2,2,128,6]{3,1,0,2:T(2,128)(2,1)}), bf16[2,2,128,6]{3,1,0,2:T(2,128)(2,1)S(1)}, u32[]{:S(2)}, u32[]{:S(2)}) async-start(bf16[2,2,128,6]{3,1,0,2:T(2,128)(2,1)} %copy.56), calls=%async_computation.2 | async-start | bytes 262144 | tf_op jit(solution)/shard_map/all_to_all | solution.py:77
  70.1 15.3 %copy-start.13 = (f32[6]{0:T(128)S(1)}, f32[6]{0:T(128)}, u32[]{:S(2)}) copy-start(f32[6]{0:T(128)} %param.17) | copy-start | bytes 76
  79.1 15.5 %all-to-all-start.1 = ((bf16[2,2,128,256]{3,1,0,2:T(2,128)(2,1)}), bf16[2,2,128,256]{3,1,0,2:T(2,128)(2,1)}, u32[]{:S(2)}, u32[]{:S(2)}) async-start(bf16[2,2,128,256]{3,1,0,2:T(2,128)(2,1)} %copy.52), calls=%async_computation.1 | async-start | bytes 524288 | tf_op jit(solution)/shard_map/all_to_all | solution.py:76
  94.7 18.4 %all-to-all-start = ((bf16[2,2,128,384]{3,1,0,2:T(2,128)(2,1)}), bf16[2,2,128,384]{3,1,0,2:T(2,128)(2,1)S(1)}, u32[]{:S(2)}, u32[]{:S(2)}) async-start(bf16[2,2,128,384]{3,1,0,2:T(2,128)(2,1)} %copy.50), calls=%async_computation | async-start | bytes 786432 | tf_op jit(solution)/shard_map/all_to_all | solution.py:75
  106.5 8.5 %copy-start.5 = (pred[128,128]{1,0:T(8,128)(4,1)S(1)}, pred[128,128]{1,0:T(8,128)(4,1)}, u32[]{:S(2)}) copy-start(pred[128,128]{1,0:T(8,128)(4,1)} %get-tuple-element.14) | copy-start | bytes 49156
  106.5 8.5 %copy-start.6 = (pred[128,128]{1,0:T(8,128)(4,1)S(1)}, pred[128,128]{1,0:T(8,128)(4,1)}, u32[]{:S(2)}) copy-start(pred[128,128]{1,0:T(8,128)(4,1)} %get-tuple-element.15) | copy-start | bytes 49156
  117.5 11.7 %copy-start.8 = (f32[6]{0:T(128)S(1)}, f32[6]{0:T(128)}, u32[]{:S(2)}) copy-start(f32[6]{0:T(128)} %copy-done.7) | copy-start | bytes 76
  118.6 20.9 %all-to-all-start.3 = ((bf16[2,128,2,384]{3,2,0,1:T(2,128)(2,1)}), bf16[2,128,2,384]{3,2,0,1:T(2,128)(2,1)S(1)}, u32[]{:S(2)}, u32[]{:S(2)}) async-start(bf16[2,128,2,384]{3,2,0,1:T(2,128)(2,1)} %copy.62), calls=%async_computation.3 | async-start | bytes 786432 | tf_op jit(solution)/shard_map/all_to_all | solution.py:79
  129.2 78.8 %reduce-scatter.2.cloned.1.call-start = ((), (), s32[]{:S(2)}) async-start(), calls=%async_computation.5 | async-start | bytes 4718592 | tf_op jit(solution)/shard_map/reduce_scatter | solution.py:88
  140.2 1.7 copy-start.10
  141.9 1.6 copy-start.11
  146.8 61.2 %copy-start.3 = (f32[2,2,128,256]{3,2,1,0:T(8,128)S(1)}, f32[2,2,128,256]{3,2,1,0:T(8,128)}, u32[]{:S(2)}) copy-start(f32[2,2,128,256]{3,2,1,0:T(8,128)} %param.10) | copy-start | bytes 1572868
Sparse Core Ops, SparseCore 0:
  9.5 42.9 all-gather.2
  146.9 61.0 reduce-scatter.1
